TPU v7x, 32 devices: a whole 2x2x4 slice. The times are simulated.
32 devices in a mesh: dp: 4 (over z), rows: 8 (over y, x, core).
Axes of the slice: x: 2, y: 2, z: 4, core: 2. Of those that a mesh axis runs over, the one named last changes fastest.
Arguments:
- latent: bfloat16 [8, 8, 64, 640], P('dp', 'rows'), may hold values from -16.25 to 16.25
- hidden: bfloat16 [8, 8, 64, 640], P('dp', 'rows'), may hold values from -16.25 to 16.25
- cotangent: bfloat16 [8, 8, 64, 640], P('dp', 'rows'), may hold values from -6 to 6
- filter_one: bfloat16 [9, 640, 640], P(None, 'dp', 'rows'), may hold values from -0.078125 to 0.078125
- filter_two: bfloat16 [9, 640, 640], P(None, 'dp', 'rows'), may hold values from -0.078125 to 0.078125
- gain_one: float32 [640], replicated, may hold values from 0.1 to 1.9
- shift_one: float32 [640], replicated, may hold values from -2.5 to 2.5
- gain_two: float32 [640], replicated, may hold values from 0.1 to 1.9
- shift_two: float32 [640], replicated, may hold values from -2.5 to 2.5
Outputs:
- latent_grad: bfloat16 [8, 8, 64, 640], P('dp', 'rows')
All inputs are finite; a program needn't handle non-finite values.
Results may differ from a plain program's by a relative error of at most 0.0027.
Values may be sent and summed in bfloat16 or wider, within the bound.
A program may use at most 128 MiB of HBM per device.

v0:
```python
import jax
import jax.numpy as jnp
from jax import lax
from jax.sharding import PartitionSpec as P

GROUPS = 16
GSIZE = 40


def extended(block, sides, width):
    for axis, dim in sides:
        count = lax.axis_size(axis)
        forward = [(i, i + 1) for i in range(count - 1)]
        backward = [(target, source) for source, target in forward]
        low = lax.ppermute(
            lax.slice_in_dim(block, block.shape[dim] - width, None, axis=dim), axis, forward
        )
        high = lax.ppermute(lax.slice_in_dim(block, 0, width, axis=dim), axis, backward)
        block = jnp.concatenate([low, block, high], axis=dim)
    return block


def group_sums(values):
    per_channel = jnp.sum(values, axis=(1, 2))
    return jnp.sum(per_channel.reshape(per_channel.shape[0], GROUPS, -1), axis=2)


def expand_groups(moment):
    return jnp.repeat(moment, GSIZE, axis=1)[:, None, None, :]


def finish_stats(sum_plain, sum_square, number):
    average = sum_plain / number
    variance = sum_square / number - average * average
    return (average, lax.rsqrt(variance + 1e-05))


def reduced_stats(field, number):
    values = field.astype(jnp.float32)
    sum_plain, sum_square = lax.psum((group_sums(values), group_sums(values * values)), "rows")
    return finish_stats(sum_plain, sum_square, number)


def norm_backward(field, stats, gain, shift, incoming, number):
    average, inverse = stats
    values = field.astype(jnp.float32)
    normed = (values - expand_groups(average)) * expand_groups(inverse)
    linear = normed * gain + shift
    logistic = jax.nn.sigmoid(linear)
    scaled = incoming * logistic * (1.0 + linear * (1.0 - logistic)) * gain
    sum_first, sum_second = lax.psum((group_sums(scaled), group_sums(scaled * normed)), "rows")
    first = sum_first / number
    second = sum_second / number
    return expand_groups(inverse) * (scaled - expand_groups(first) - normed * expand_groups(second))


def conv_backward(gradient, weights):
    images, rows_here, breadth, channels = gradient.shape
    padded = extended(gradient, (("rows", 1),), 1)
    padded = jnp.pad(padded, ((0, 0), (0, 0), (1, 1), (0, 0)))
    pixels = images * rows_here * breadth
    shifted = []
    for tap_index in range(9):
        down_step = tap_index // 3 - 1
        side_step = tap_index % 3 - 1
        window = padded[
            :, 1 - down_step : 1 - down_step + rows_here, 1 - side_step : 1 - side_step + breadth, :
        ]
        shifted.append(window.reshape(pixels, channels))
    stacked = jnp.stack(shifted, axis=1)
    gathered = lax.all_gather(weights, "dp", axis=1, tiled=True)
    section = lax.all_gather(gathered, "rows", axis=2, tiled=True)
    columns = section.shape[2]
    window = stacked.reshape(pixels, 9 * columns)
    flat = jnp.transpose(section, (0, 2, 1)).reshape(9 * columns, section.shape[1])
    result = jnp.dot(window, flat, preferred_element_type=jnp.float32)
    return result.reshape(images, rows_here, breadth, channels)


def body(
    latent, hidden, cotangent, filter_one, filter_two, gain_one, shift_one, gain_two, shift_two
):
    number = latent.shape[1] * lax.axis_size("rows") * latent.shape[2] * GSIZE
    stats_two = reduced_stats(hidden, number)
    back_two = conv_backward(cotangent, filter_two)
    hidden_grad = norm_backward(hidden, stats_two, gain_two, shift_two, back_two, number).astype(
        jnp.bfloat16
    )
    stats_one = reduced_stats(latent, number)
    back_one = conv_backward(hidden_grad, filter_one)
    latent_part = norm_backward(latent, stats_one, gain_one, shift_one, back_one, number)
    return (cotangent.astype(jnp.float32) + latent_part).astype(jnp.bfloat16)


def solution(mesh):
    in_specs = (
        P("dp", "rows", None, None),
        P("dp", "rows", None, None),
        P("dp", "rows", None, None),
        P(None, "dp", "rows"),
        P(None, "dp", "rows"),
        P(),
        P(),
        P(),
        P(),
    )
    out_specs = P("dp", "rows", None, None)
    return jax.shard_map(body, mesh=mesh, in_specs=in_specs, out_specs=out_specs, check_vma=False)
```

profile of v0, /device:TPU:28, one launch (start us, length us, event | category | flops | bytes accessed | tf_op | source)
XLA Modules:
  0.0 223.1 jit_solution(1200964164859489196)
XLA Ops:
  6.5 1.2 copy.112
  7.7 47.0 %all_gather.12 = bf16[9,640,80]{2,0,1:T(8,128)(2,1)S(1)} all-gather(bf16[9,160,80]{2,0,1:T(8,128)(2,1)S(1)} %copy.112), channel_id=1, replica_groups=mesh['dp'=4,'rows'=8] {'dp'}, dimensions={1}, use_global_device_ids=true | all-gather | bytes 1152000 | tf_op jit(solution)/shard_map/all_gather | solution.py:71
  54.7 3.0 %copy.113 = bf16[9,640,80]{1,2,0:T(8,128)(2,1)} copy(bf16[9,640,80]{2,0,1:T(8,128)(2,1)S(1)} %all_gather.12) | data formatting | bytes 1843200 | tf_op jit(solution)/shard_map/all_gather | solution.py:71
  58.0 45.9 %all_gather.14 = bf16[9,640,80]{2,0,1:T(8,128)(2,1)S(1)} all-gather(bf16[9,160,80]{2,0,1:T(8,128)(2,1)S(1)} %copy.123), channel_id=1, replica_groups=mesh['dp'=4,'rows'=8] {'dp'}, dimensions={1}, use_global_device_ids=true | all-gather | bytes 1152000 | tf_op jit(solution)/shard_map/all_gather | solution.py:71
  103.8 3.0 %copy.124 = bf16[9,640,80]{1,2,0:T(8,128)(2,1)} copy(bf16[9,640,80]{2,0,1:T(8,128)(2,1)S(1)} %all_gather.14) | data formatting | bytes 1843200 | tf_op jit(solution)/shard_map/all_gather | solution.py:71
  106.9 2.1 collective-permute-start
  108.9 4.5 %collective-permute-start.1 = (bf16[2,1,64,640]{3,2,1,0:T(8,128)(2,1)S(1)}, bf16[2,1,64,640]{3,2,1,0:T(8,128)(2,1)S(1)}, u32[]{:S(2)}, u32[]{:S(2)}) collective-permute-start(bf16[2,1,64,640]{3,2,1,0:T(8,128)(2,1)S(1)} %copy-done), channel_id=1, source_target_pairs={{1,0},{2,1},{3,2},{4,3},{5,4},{6,5},{7,6},{9,8},{10,9},{11,10},{12... | collective-permute-start | bytes 491528 | tf_op jit(solution)/shard_map/ppermute | solution.py:18
  113.9 12.3 %all-reduce.4 = (f32[2,16]{1,0:T(2,128)S(1)}, f32[2,16]{1,0:T(2,128)S(1)}) all-reduce(f32[2,16]{1,0:T(2,128)S(1)} %reduce_sum.151, f32[2,16]{1,0:T(2,128)S(1)} %reduce_sum.149), channel_id=1, replica_groups=mesh['dp'=4,'rows'=8] {'rows'}, use_global_device_ids=true, to_apply=%region_11.12 | all-reduce | flops 64 | bytes 512 | tf_op jit(solution)/shard_map/psum | solution.py:40
  127.9 1.0 copy.105
  129.8 1.0 copy.108
  130.8 1.0 copy.109
  131.8 1.0 copy.111
  132.8 1.0 copy.104
  133.8 1.0 copy.110
  134.8 11.1 %stack.6 = bf16[128,9,640]{2,1,0:T(8,128)(2,1)S(1)} concatenate(bf16[128,1,640]{2,1,0:T(2,128)(2,1)S(1)} %copy.103, bf16[128,1,640]{2,1,0:T(2,128)(2,1)} %copy.104, bf16[128,1,640]{2,1,0:T(2,128)(2,1)} %copy.105, bf16[128,1,640]{2,1,0:T(2,128)(2,1)} %copy.106, bf16[128,1,640]{2,1,0:T(2,128)(2,1)S(1)} %copy.107, bf16[128,1,640]{2,1,0:T(2,128)(2,1)} %copy.108, ...), dimensions={1} | concatenate | bytes 2949120 | tf_op jit(solution)/shard_map/stack | solution.py:70
  145.9 1.8 reshape.88
  147.7 5.1 %fusion.53 = (f32[2,640]{1,0:T(2,128)S(1)}, f32[2,640]{1,0:T(2,128)S(1)}, f32[2,1,64,640]{3,2,0,1:T(8,128)S(1)}) fusion(f32[2,640]{1,0:T(2,128)S(1)} %mul.122, f32[2,640]{1,0:T(2,128)S(1)} %sub.60, bf16[2,1,64,640]{3,2,1,0:T(8,128)(2,1)S(1)} %copy-done.4, f32[640]{0:T(1024)S(1)} %copy-done.6, f32[640]{0:T(1024)S(1)} %copy-done.7, ...), kind=kOutput, calls=%fused_computation.73 | convolution fusion | flops 945108480 | bytes 9364480 | tf_op jit(solution)/shard_map/dot_general | solution.py:76
  153.1 12.0 %all-reduce.3 = (f32[2,16]{1,0:T(2,128)S(1)}, f32[2,16]{1,0:T(2,128)S(1)}, f32[2,16]{1,0:T(2,128)S(1)}, f32[2,16]{1,0:T(2,128)S(1)}) all-reduce(f32[2,16]{1,0:T(2,128)S(1)} %reduce_sum.155, f32[2,16]{1,0:T(2,128)S(1)} %reduce_sum.153, f32[2,16]{1,0:T(2,128)S(1)} %reduce_sum.147, ...), channel_id=1, replica_groups=mesh['dp'=4,'rows'=8] {'rows'}, use_global_device_ids=true, to_apply=%region_17.18 | all-reduce | flops 128 | bytes 1024 | tf_op jit(solution)/shard_map/psum | solution.py:51
  165.5 1.9 collective-permute-start.2
  167.5 4.7 %collective-permute-start.3 = (bf16[2,1,64,640]{3,2,0,1:T(8,128)(2,1)S(1)}, bf16[2,1,64,640]{3,2,0,1:T(8,128)(2,1)S(1)}, u32[]{:S(2)}, u32[]{:S(2)}) collective-permute-start(bf16[2,1,64,640]{3,2,0,1:T(8,128)(2,1)S(1)} %fusion.50), channel_id=1, source_target_pairs={{1,0},{2,1},{3,2},{4,3},{5,4},{6,5},{7,6},{9,8},{10,9},{11,10},{12... | collective-permute-start | bytes 491528 | tf_op jit(solution)/shard_map/ppermute | solution.py:18
  172.8 1.2 collective-permute-done.2
  175.4 1.0 copy.116
  176.4 1.0 copy.117
  177.4 1.0 copy.119
  178.4 1.0 copy.120
  179.4 1.0 copy.122
  180.3 1.0 copy.115
  181.3 1.0 copy.121
  182.3 11.0 %stack.7 = bf16[128,9,640]{2,1,0:T(8,128)(2,1)S(1)} concatenate(bf16[128,1,640]{2,1,0:T(2,128)(2,1)S(1)} %copy.114, bf16[128,1,640]{2,1,0:T(2,128)(2,1)} %copy.115, bf16[128,1,640]{2,1,0:T(2,128)(2,1)} %copy.116, bf16[128,1,640]{2,1,0:T(2,128)(2,1)} %copy.117, bf16[128,1,640]{2,1,0:T(2,128)(2,1)S(1)} %copy.118, bf16[128,1,640]{2,1,0:T(2,128)(2,1)} %copy.119, ...), dimensions={1} | concatenate | bytes 2949120 | tf_op jit(solution)/shard_map/stack | solution.py:70
  193.4 1.8 reshape.92
  195.2 4.9 %fusion.52 = (f32[2,640]{1,0:T(2,128)S(1)}, f32[2,640]{1,0:T(2,128)S(1)}, f32[2,1,64,640]{3,2,0,1:T(8,128)S(1)}) fusion(f32[2,640]{1,0:T(2,128)S(1)} %mul.118, f32[2,640]{1,0:T(2,128)S(1)} %sub.68, bf16[2,1,64,640]{3,2,1,0:T(8,128)(2,1)S(1)} %copy-done.2, f32[640]{0:T(1024)S(1)} %copy-done.8, f32[640]{0:T(1024)S(1)} %copy-done.9, ...), kind=kOutput, calls=%fused_computation.72 | convolution fusion | flops 945108480 | bytes 9364480 | tf_op jit(solution)/shard_map/dot_general | solution.py:76
  200.5 14.6 %all-reduce.2 = (f32[2,16]{1,0:T(2,128)S(1)}, f32[2,16]{1,0:T(2,128)S(1)}) all-reduce(f32[2,16]{1,0:T(2,128)S(1)} %reduce_sum.159, f32[2,16]{1,0:T(2,128)S(1)} %reduce_sum.157), channel_id=1, replica_groups=mesh['dp'=4,'rows'=8] {'rows'}, use_global_device_ids=true, to_apply=%region_23.24 | all-reduce | flops 64 | bytes 512 | tf_op jit(solution)/shard_map/psum | solution.py:51
  (80 shorter events, 7.5 us)
Async XLA Ops:
  6.5 141.2 %all-gather.3.cloned.1.call-start = ((), (), s32[]{:S(2)}) async-start(), calls=%async_computation | async-start | bytes 8294400 | tf_op jit(solution)/shard_map/all_gather | solution.py:72
  54.7 3.1 %copy-start.5 = (bf16[9,160,80]{2,1,0:T(8,128)(2,1)S(1)}, bf16[9,160,80]{2,1,0:T(8,128)(2,1)}, u32[]{:S(2)}) copy-start(bf16[9,160,80]{2,1,0:T(8,128)(2,1)} %param.12) | copy-start | bytes 691204
  57.7 137.5 %all-gather.5.cloned.1.call-start = ((), (), s32[]{:S(2)}) async-start(), calls=%async_computation.1 | async-start | bytes 8294400 | tf_op jit(solution)/shard_map/all_gather | solution.py:72
  103.8 3.0 %copy-start = (bf16[2,1,64,640]{3,2,1,0:T(8,128)(2,1)S(1)}, bf16[2,1,64,640]{3,2,1,0:T(8,128)(2,1)}, u32[]{:S(2)}) copy-start(bf16[2,1,64,640]{3,2,1,0:T(8,128)(2,1)} %param.11) | copy-start | bytes 491524
  103.8 9.6 %copy-start.3 = (bf16[2,1,64,640]{3,2,1,0:T(8,128)(2,1)S(1)}, bf16[2,1,64,640]{3,2,1,0:T(8,128)(2,1)}, u32[]{:S(2)}) copy-start(bf16[2,1,64,640]{3,2,1,0:T(8,128)(2,1)} %param.10) | copy-start | bytes 491524
  106.8 20.0 %copy-start.1 = (bf16[2,1,64,640]{3,2,1,0:T(8,128)(2,1)S(1)}, bf16[2,1,64,640]{3,2,1,0:T(8,128)(2,1)}, u32[]{:S(2)}) copy-start(bf16[2,1,64,640]{3,2,1,0:T(8,128)(2,1)} %param.9) | copy-start | bytes 491524
  106.9 20.4 %collective-permute-start = (bf16[2,1,64,640]{3,2,1,0:T(8,128)(2,1)S(1)}, bf16[2,1,64,640]{3,2,1,0:T(8,128)(2,1)S(1)}, u32[]{:S(2)}, u32[]{:S(2)}) collective-permute-start(bf16[2,1,64,640]{3,2,1,0:T(8,128)(2,1)S(1)} %copy-done), channel_id=1, source_target_pairs={{0,1},{1,2},{2,3},{3,4},{4,5},{5,6},{6,7},{8,9},{9,10},{10,11},{11... | collective-permute-start | bytes 491528 | tf_op jit(solution)/shard_map/ppermute | solution.py:15
  108.9 18.4 %collective-permute-start.1 = (bf16[2,1,64,640]{3,2,1,0:T(8,128)(2,1)S(1)}, bf16[2,1,64,640]{3,2,1,0:T(8,128)(2,1)S(1)}, u32[]{:S(2)}, u32[]{:S(2)}) collective-permute-start(bf16[2,1,64,640]{3,2,1,0:T(8,128)(2,1)S(1)} %copy-done), channel_id=1, source_target_pairs={{1,0},{2,1},{3,2},{4,3},{5,4},{6,5},{7,6},{9,8},{10,9},{11,10},{12... | collective-permute-start | bytes 491528 | tf_op jit(solution)/shard_map/ppermute | solution.py:18
  145.9 1.8 copy-start.4
  145.9 1.8 copy-start.6
  145.9 1.8 copy-start.7
  165.5 8.4 %collective-permute-start.2 = (bf16[2,1,64,640]{3,2,0,1:T(8,128)(2,1)S(1)}, bf16[2,1,64,640]{3,2,0,1:T(8,128)(2,1)S(1)}, u32[]{:S(2)}, u32[]{:S(2)}) collective-permute-start(bf16[2,1,64,640]{3,2,0,1:T(8,128)(2,1)S(1)} %fusion.50), channel_id=1, source_target_pairs={{0,1},{1,2},{2,3},{3,4},{4,5},{5,6},{6,7},{8,9},{9,10},{10,11},{11... | collective-permute-start | bytes 491528 | tf_op jit(solution)/shard_map/ppermute | solution.py:15
  167.5 7.4 %collective-permute-start.3 = (bf16[2,1,64,640]{3,2,0,1:T(8,128)(2,1)S(1)}, bf16[2,1,64,640]{3,2,0,1:T(8,128)(2,1)S(1)}, u32[]{:S(2)}, u32[]{:S(2)}) collective-permute-start(bf16[2,1,64,640]{3,2,0,1:T(8,128)(2,1)S(1)} %fusion.50), channel_id=1, source_target_pairs={{1,0},{2,1},{3,2},{4,3},{5,4},{6,5},{7,6},{9,8},{10,9},{11,10},{12... | collective-permute-start | bytes 491528 | tf_op jit(solution)/shard_map/ppermute | solution.py:18
  193.4 1.8 copy-start.2
  193.4 1.8 copy-start.8
  193.4 1.8 copy-start.9
Sparse Core Ops, SparseCore 0:
  57.9 50.5 all-gather.2
  110.4 50.1 all-gather.4
where the time goes:
time: 225 us; the launch traced here: 223 us
  blocking collectives  132 us (59%)
  local copies, waits for them, and re-layouts  50.2 us (22%)
  between operations  13.8 us (6%)
  starting transfers between devices  13.3 us (6%)
  matrix products  10 us (4%)
    all_gather x2, blocking collectives, conv_backward(): gathered = lax.all_gather(weights, 'dp', axis=1, tiled=True)  92.9 us
    another operation x20, local copies, waits for them, and re-layouts, conv_backward(): stacked = jnp.stack(shifted, axis=1)  36.9 us
    psum x2, blocking collectives, norm_backward(): lax.psum((group_sums(scaled), group_sums(scaled * normed)), 'rows')  26.5 us
    psum x1, blocking collectives, reduced_stats(): lax.psum((group_sums(values), group_sums(values * values)), 'rows')  12.3 us
    dot_general x2, matrix products, conv_backward(): result = jnp.dot(window, flat, preferred_element_type=jnp.float32)  10 us
    ppermute x2, starting transfers between devices, extended(): lax.ppermute(lax.slice_in_dim(block, 0, width, axis=dim), axis, backward)  9.26 us
    all_gather x2, local copies, waits for them, and re-layouts, conv_backward(): gathered = lax.all_gather(weights, 'dp', axis=1, tiled=True)  5.97 us
  transfers between devices with their start and end apart: 6, of which 2 were waited for; matrix products, arithmetic and copies ran while one was open for 23% of the time, Pallas kernels for 0%

commit v1 on v0

--- a/solution.py
+++ b/solution.py
@@ -68,7 +68,7 @@
         ]
         shifted.append(window.reshape(pixels, channels))
     stacked = jnp.stack(shifted, axis=1)
-    gathered = lax.all_gather(weights, "dp", axis=1, tiled=True)
+    gathered = jnp.concatenate(lax.all_gather(weights, axis_name="dp"), axis=1)
     section = lax.all_gather(gathered, "rows", axis=2, tiled=True)
     columns = section.shape[2]
     window = stacked.reshape(pixels, 9 * columns)

time: 225 us -> 195 us (0.87)
  blocking collectives: 132 us -> 99.8 us
  waiting for transfers between devices: 2.08 us -> 5.66 us
    all_gather x2, blocking collectives: 92.9 us -> 56.6 us  [conv_backward(): gathered = jnp.concatenate(lax.all_gather(weights, axis_name='dp'), axis=1)]
    all_gather x2 -> x0, local copies, waits for them, and re-layouts: 5.97 us -> none  [conv_backward(): gathered = lax.all_gather(weights, 'dp', axis=1, tiled=True)]
    reshape x0 -> x4, local copies, waits for them, and re-layouts: none -> 5.67 us  [conv_backward(): gathered = jnp.concatenate(lax.all_gather(weights, axis_name='dp'), axis=1)]
    ppermute x2, waiting for transfers between devices: 1.18 us -> 5.62 us  [extended(): lax.ppermute(lax.slice_in_dim(block, block.shape[dim] - width, None, axis...]
    psum x1, blocking collectives: 12.3 us -> 16.5 us  [reduced_stats(): lax.psum((group_sums(values), group_sums(values * values)), 'rows')]
  transfers between devices with their start and end apart: 6 -> 6, of which waited for: 2 -> 1; matrix products, arithmetic and copies ran while one was open for 23% -> 27% of each run, Pallas kernels for 0% -> 0%
where the time goes in v1:
time: 195 us; the launch traced here: 193 us
  blocking collectives  99.8 us (51%)
  local copies, waits for them, and re-layouts  48.5 us (25%)
  between operations  13.8 us (7%)
  starting transfers between devices  13.3 us (7%)
  matrix products  9.89 us (5%)
  waiting for transfers between devices  5.66 us (3%)
  other arithmetic  2.04 us (1%)
    all_gather x2, blocking collectives, conv_backward(): gathered = jnp.concatenate(lax.all_gather(weights, axis_name='dp'), axis=1)  56.6 us
    another operation x20, local copies, waits for them, and re-layouts, conv_backward(): stacked = jnp.stack(shifted, axis=1)  36.9 us
    psum x2, blocking collectives, norm_backward(): lax.psum((group_sums(scaled), group_sums(scaled * normed)), 'rows')  26.6 us
    psum x1, blocking collectives, reduced_stats(): lax.psum((group_sums(values), group_sums(values * values)), 'rows')  16.5 us
    dot_general x2, matrix products, conv_backward(): result = jnp.dot(window, flat, preferred_element_type=jnp.float32)  9.89 us
    ppermute x2, starting transfers between devices, extended(): lax.ppermute(lax.slice_in_dim(block, 0, width, axis=dim), axis, backward)  9.26 us
    reshape x4, local copies, waits for them, and re-layouts, conv_backward(): gathered = jnp.concatenate(lax.all_gather(weights, axis_name='dp'), axis=1)  5.67 us
    ppermute x2, waiting for transfers between devices, extended(): lax.ppermute(lax.slice_in_dim(block, block.shape[dim] - width, None, axis...  5.62 us
  transfers between devices with their start and end apart: 6, of which 1 were waited for; matrix products, arithmetic and copies ran while one was open for 27% of the time, Pallas kernels for 0%

profile of v1, /device:TPU:28, one launch (start us, length us, event | category | flops | bytes accessed | tf_op | source)
XLA Modules:
  0.0 192.9 jit_solution(15293250995902167997)
XLA Ops:
  6.5 28.8 %all-gather = bf16[36,160,80]{2,1,0:T(8,128)(2,1)S(1)} all-gather(bf16[9,160,80]{2,1,0:T(8,128)(2,1)} %param.13), channel_id=2, replica_groups=mesh['dp'=4,'rows'=8] {'dp'}, dimensions={0}, use_global_device_ids=true | all-gather | bytes 1152000 | tf_op jit(solution)/shard_map/all_gather | solution.py:71
  35.3 1.1 copy.86
  36.5 1.7 reshape.102
  38.2 27.9 %all-gather.1 = bf16[36,160,80]{2,1,0:T(8,128)(2,1)S(1)} all-gather(bf16[9,160,80]{2,1,0:T(8,128)(2,1)S(1)} %copy-done.5), channel_id=3, replica_groups=mesh['dp'=4,'rows'=8] {'dp'}, dimensions={0}, use_global_device_ids=true | all-gather | bytes 1152000 | tf_op jit(solution)/shard_map/all_gather | solution.py:71
  66.1 1.1 copy.96
  67.3 1.7 reshape.108
  69.0 2.1 %collective-permute-start = (bf16[2,1,64,640]{3,2,1,0:T(8,128)(2,1)S(1)}, bf16[2,1,64,640]{3,2,1,0:T(8,128)(2,1)S(1)}, u32[]{:S(2)}, u32[]{:S(2)}) collective-permute-start(bf16[2,1,64,640]{3,2,1,0:T(8,128)(2,1)S(1)} %copy-done), channel_id=1, source_target_pairs={{0,1},{1,2},{2,3},{3,4},{4,5},{5,6},{6,7},{8,9},{9,10},{10,11},{11... | collective-permute-start | bytes 491528 | tf_op jit(solution)/shard_map/ppermute | solution.py:15
  71.1 4.5 %collective-permute-start.1 = (bf16[2,1,64,640]{3,2,1,0:T(8,128)(2,1)S(1)}, bf16[2,1,64,640]{3,2,1,0:T(8,128)(2,1)S(1)}, u32[]{:S(2)}, u32[]{:S(2)}) collective-permute-start(bf16[2,1,64,640]{3,2,1,0:T(8,128)(2,1)S(1)} %copy-done), channel_id=1, source_target_pairs={{1,0},{2,1},{3,2},{4,3},{5,4},{6,5},{7,6},{9,8},{10,9},{11,10},{12... | collective-permute-start | bytes 491528 | tf_op jit(solution)/shard_map/ppermute | solution.py:18
  76.1 16.5 %all-reduce.4 = (f32[2,16]{1,0:T(2,128)S(1)}, f32[2,16]{1,0:T(2,128)S(1)}) all-reduce(f32[2,16]{1,0:T(2,128)S(1)} %reduce_sum.151, f32[2,16]{1,0:T(2,128)S(1)} %reduce_sum.149), channel_id=1, replica_groups=mesh['dp'=4,'rows'=8] {'rows'}, use_global_device_ids=true, to_apply=%region_11.12 | all-reduce | flops 64 | bytes 512 | tf_op jit(solution)/shard_map/psum | solution.py:40
  96.2 1.0 copy.82
  97.1 1.0 copy.83
  98.1 1.0 copy.85
  99.1 1.0 copy.78
  100.1 1.0 copy.84
  101.1 11.1 %stack.6 = bf16[128,9,640]{2,1,0:T(8,128)(2,1)S(1)} concatenate(bf16[128,1,640]{2,1,0:T(2,128)(2,1)S(1)} %copy.77, bf16[128,1,640]{2,1,0:T(2,128)(2,1)} %copy.78, bf16[128,1,640]{2,1,0:T(2,128)(2,1)} %copy.79, bf16[128,1,640]{2,1,0:T(2,128)(2,1)} %copy.80, bf16[128,1,640]{2,1,0:T(2,128)(2,1)S(1)} %copy.81, bf16[128,1,640]{2,1,0:T(2,128)(2,1)} %copy.82, ...), dimensions={1} | concatenate | bytes 2949120 | tf_op jit(solution)/shard_map/stack | solution.py:70
  112.2 1.8 reshape.100
  114.0 5.0 %fusion.53 = (f32[2,640]{1,0:T(2,128)S(1)}, f32[2,640]{1,0:T(2,128)S(1)}, f32[2,1,64,640]{3,2,0,1:T(8,128)S(1)}) fusion(f32[2,640]{1,0:T(2,128)S(1)} %mul.122, f32[2,640]{1,0:T(2,128)S(1)} %sub.60, bf16[2,1,64,640]{3,2,1,0:T(8,128)(2,1)S(1)} %copy-done.4, f32[640]{0:T(1024)S(1)} %copy-done.6, f32[640]{0:T(1024)S(1)} %copy-done.7, ...), kind=kOutput, calls=%fused_computation.73 | convolution fusion | flops 945108480 | bytes 9364480 | tf_op jit(solution)/shard_map/dot_general | solution.py:76
  119.3 12.6 %all-reduce.3 = (f32[2,16]{1,0:T(2,128)S(1)}, f32[2,16]{1,0:T(2,128)S(1)}, f32[2,16]{1,0:T(2,128)S(1)}, f32[2,16]{1,0:T(2,128)S(1)}) all-reduce(f32[2,16]{1,0:T(2,128)S(1)} %reduce_sum.155, f32[2,16]{1,0:T(2,128)S(1)} %reduce_sum.153, f32[2,16]{1,0:T(2,128)S(1)} %reduce_sum.147, ...), channel_id=1, replica_groups=mesh['dp'=4,'rows'=8] {'rows'}, use_global_device_ids=true, to_apply=%region_17.18 | all-reduce | flops 128 | bytes 1024 | tf_op jit(solution)/shard_map/psum | solution.py:51
  132.4 1.9 collective-permute-start.2
  134.3 4.7 %collective-permute-start.3 = (bf16[2,1,64,640]{3,2,0,1:T(8,128)(2,1)S(1)}, bf16[2,1,64,640]{3,2,0,1:T(8,128)(2,1)S(1)}, u32[]{:S(2)}, u32[]{:S(2)}) collective-permute-start(bf16[2,1,64,640]{3,2,0,1:T(8,128)(2,1)S(1)} %fusion.50), channel_id=1, source_target_pairs={{1,0},{2,1},{3,2},{4,3},{5,4},{6,5},{7,6},{9,8},{10,9},{11,10},{12... | collective-permute-start | bytes 491528 | tf_op jit(solution)/shard_map/ppermute | solution.py:18
  139.6 5.6 %collective-permute-done.2 = bf16[2,1,64,640]{3,2,0,1:T(8,128)(2,1)S(1)} collective-permute-done((bf16[2,1,64,640]{3,2,0,1:T(8,128)(2,1)S(1)}, bf16[2,1,64,640]{3,2,0,1:T(8,128)(2,1)S(1)}, u32[]{:S(2)}, u32[]{:S(2)}) %collective-permute-start.2) | collective-permute-done | bytes 163872 | tf_op jit(solution)/shard_map/ppermute | solution.py:15
  145.8 1.0 copy.89
  146.8 1.0 copy.90
  147.8 1.0 copy.92
  148.8 1.0 copy.93
  149.8 1.0 copy.95
  150.7 1.0 copy.88
  151.7 1.0 copy.94
  152.7 11.0 %stack.7 = bf16[128,9,640]{2,1,0:T(8,128)(2,1)S(1)} concatenate(bf16[128,1,640]{2,1,0:T(2,128)(2,1)S(1)} %copy.87, bf16[128,1,640]{2,1,0:T(2,128)(2,1)} %copy.88, bf16[128,1,640]{2,1,0:T(2,128)(2,1)} %copy.89, bf16[128,1,640]{2,1,0:T(2,128)(2,1)} %copy.90, bf16[128,1,640]{2,1,0:T(2,128)(2,1)S(1)} %copy.91, bf16[128,1,640]{2,1,0:T(2,128)(2,1)} %copy.92, ...), dimensions={1} | concatenate | bytes 2949120 | tf_op jit(solution)/shard_map/stack | solution.py:70
  163.8 1.8 reshape.106
  165.6 4.9 %fusion.52 = (f32[2,640]{1,0:T(2,128)S(1)}, f32[2,640]{1,0:T(2,128)S(1)}, f32[2,1,64,640]{3,2,0,1:T(8,128)S(1)}) fusion(f32[2,640]{1,0:T(2,128)S(1)} %mul.118, f32[2,640]{1,0:T(2,128)S(1)} %sub.68, bf16[2,1,64,640]{3,2,1,0:T(8,128)(2,1)S(1)} %copy-done.2, f32[640]{0:T(1024)S(1)} %copy-done.8, f32[640]{0:T(1024)S(1)} %copy-done.9, ...), kind=kOutput, calls=%fused_computation.72 | convolution fusion | flops 945108480 | bytes 9364480 | tf_op jit(solution)/shard_map/dot_general | solution.py:76
  170.9 14.0 %all-reduce.2 = (f32[2,16]{1,0:T(2,128)S(1)}, f32[2,16]{1,0:T(2,128)S(1)}) all-reduce(f32[2,16]{1,0:T(2,128)S(1)} %reduce_sum.159, f32[2,16]{1,0:T(2,128)S(1)} %reduce_sum.157), channel_id=1, replica_groups=mesh['dp'=4,'rows'=8] {'rows'}, use_global_device_ids=true, to_apply=%region_23.24 | all-reduce | flops 64 | bytes 512 | tf_op jit(solution)/shard_map/psum | solution.py:51
  (80 shorter events, 7.4 us)
Async XLA Ops:
  6.5 107.4 %all-gather.5.cloned.1.call-start = ((), (), s32[]{:S(2)}) async-start(), calls=%async_computation | async-start | bytes 8294400 | tf_op jit(solution)/shard_map/all_gather | solution.py:72
  36.4 1.8 copy-start.5
  38.2 127.4 %all-gather.7.cloned.1.call-start = ((), (), s32[]{:S(2)}) async-start(), calls=%async_computation.1 | async-start | bytes 8294400 | tf_op jit(solution)/shard_map/all_gather | solution.py:72
  67.3 1.8 copy-start
  67.3 8.4 %copy-start.3 = (bf16[2,1,64,640]{3,2,1,0:T(8,128)(2,1)S(1)}, bf16[2,1,64,640]{3,2,1,0:T(8,128)(2,1)}, u32[]{:S(2)}) copy-start(bf16[2,1,64,640]{3,2,1,0:T(8,128)(2,1)} %param.10) | copy-start | bytes 491524
  69.0 24.2 %copy-start.1 = (bf16[2,1,64,640]{3,2,1,0:T(8,128)(2,1)S(1)}, bf16[2,1,64,640]{3,2,1,0:T(8,128)(2,1)}, u32[]{:S(2)}) copy-start(bf16[2,1,64,640]{3,2,1,0:T(8,128)(2,1)} %param.9) | copy-start | bytes 491524
  69.0 24.6 %collective-permute-start = (bf16[2,1,64,640]{3,2,1,0:T(8,128)(2,1)S(1)}, bf16[2,1,64,640]{3,2,1,0:T(8,128)(2,1)S(1)}, u32[]{:S(2)}, u32[]{:S(2)}) collective-permute-start(bf16[2,1,64,640]{3,2,1,0:T(8,128)(2,1)S(1)} %copy-done), channel_id=1, source_target_pairs={{0,1},{1,2},{2,3},{3,4},{4,5},{5,6},{6,7},{8,9},{9,10},{10,11},{11... | collective-permute-start | bytes 491528 | tf_op jit(solution)/shard_map/ppermute | solution.py:15
  71.1 22.5 %collective-permute-start.1 = (bf16[2,1,64,640]{3,2,1,0:T(8,128)(2,1)S(1)}, bf16[2,1,64,640]{3,2,1,0:T(8,128)(2,1)S(1)}, u32[]{:S(2)}, u32[]{:S(2)}) collective-permute-start(bf16[2,1,64,640]{3,2,1,0:T(8,128)(2,1)S(1)} %copy-done), channel_id=1, source_target_pairs={{1,0},{2,1},{3,2},{4,3},{5,4},{6,5},{7,6},{9,8},{10,9},{11,10},{12... | collective-permute-start | bytes 491528 | tf_op jit(solution)/shard_map/ppermute | solution.py:18
  112.2 1.8 copy-start.4
  112.2 1.8 copy-start.6
  112.2 1.8 copy-start.7
  132.4 12.9 %collective-permute-start.2 = (bf16[2,1,64,640]{3,2,0,1:T(8,128)(2,1)S(1)}, bf16[2,1,64,640]{3,2,0,1:T(8,128)(2,1)S(1)}, u32[]{:S(2)}, u32[]{:S(2)}) collective-permute-start(bf16[2,1,64,640]{3,2,0,1:T(8,128)(2,1)S(1)} %fusion.50), channel_id=1, source_target_pairs={{0,1},{1,2},{2,3},{3,4},{4,5},{5,6},{6,7},{8,9},{9,10},{10,11},{11... | collective-permute-start | bytes 491528 | tf_op jit(solution)/shard_map/ppermute | solution.py:15
  134.3 10.9 %collective-permute-start.3 = (bf16[2,1,64,640]{3,2,0,1:T(8,128)(2,1)S(1)}, bf16[2,1,64,640]{3,2,0,1:T(8,128)(2,1)S(1)}, u32[]{:S(2)}, u32[]{:S(2)}) collective-permute-start(bf16[2,1,64,640]{3,2,0,1:T(8,128)(2,1)S(1)} %fusion.50), channel_id=1, source_target_pairs={{1,0},{2,1},{3,2},{4,3},{5,4},{6,5},{7,6},{9,8},{10,9},{11,10},{12... | collective-permute-start | bytes 491528 | tf_op jit(solution)/shard_map/ppermute | solution.py:18
  163.8 1.8 copy-start.2
  163.8 1.8 copy-start.8
  163.8 1.8 copy-start.9
Sparse Core Ops, SparseCore 0:
  38.3 52.6 all-gather.4
  92.9 53.3 all-gather.6
